TPU v7x, 256 devices: a whole 4x4x8 slice. The times are simulated.
256 devices in a mesh: row: 32 (over z, x), col: 8 (over y, core).
Axes of the slice: x: 4, y: 4, z: 8, core: 2. Of those that a mesh axis runs over, the one named last changes fastest.
Arguments:
- integrals: bfloat16 [65536, 8192], P('row', 'col'), may hold values from -0.0234375 to 0.0234375
- lambda2: bfloat16 [2016, 65536], P('col', 'row'), may hold values from -6 to 6
- source_terms: float32 [2016, 8192], P('row', 'col'), may hold values from -6 to 6
- hist_amp: bfloat16 [5, 2016, 8192], P(None, 'row', 'col'), may hold values from -6 to 6
- hist_err: bfloat16 [5, 2016, 8192], P(None, 'row', 'col'), may hold values from -64 to 64
- eps_occ: float32 [64], replicated, may hold values from -1 to -0.3
- eps_vir: float32 [800], replicated, may hold values from 0.1 to 1
- occ_pair: int32 [2, 2016], P(None, 'row'), may hold values from 0 to 63, as said below
- vir_pair: int32 [2, 8192], P(None, 'col'), may hold values from 0 to 799, as said below
Outputs:
- updated: float32 [2016, 8192], P('row', 'col')
Inputs may be any that keep to these rules, and one draw needn't show every extreme that they name: `occ_pair`: every pair i < j of the 64 occupied orbitals appears exactly once, in some order. `vir_pair`: in every column the first orbital is smaller than the second.
All inputs are finite; a program needn't handle non-finite values.
Results may differ from a plain program's by a relative error of at most 0.0003.
Values may be sent and summed in bfloat16 or wider, within the bound.
A program may use at most 64 MiB of HBM per device.

v0:
```python
import jax
import jax.numpy as jnp
from jax import lax
from jax.sharding import PartitionSpec as P

precise = lax.Precision.HIGHEST


def pair_energy(pairs, energies):
    levels = jnp.arange(energies.shape[0], dtype=jnp.int32)
    first = jnp.sum(jnp.where(pairs[0][:, None] == levels[None, :], energies[None, :], 0.0), axis=1)
    second = jnp.sum(
        jnp.where(pairs[1][:, None] == levels[None, :], energies[None, :], 0.0), axis=1
    )
    return first + second


def diis_weights(correlation):
    factor = jnp.linalg.cholesky(correlation)
    order = correlation.shape[0]
    forward = []
    for k in range(order):
        running = jnp.ones((), correlation.dtype)
        for m in range(k):
            running = running - factor[k, m] * forward[m]
        forward.append(running / factor[k, k])
    backward = [None] * order
    for k in reversed(range(order)):
        running = forward[k]
        for m in range(k + 1, order):
            running = running - factor[m, k] * backward[m]
        backward[k] = running / factor[k, k]
    solved = jnp.stack(backward)
    return solved / jnp.sum(solved)


def on_device(
    integrals, lambda2, source_terms, hist_amp, hist_err, eps_occ, eps_vir, occ_pair, vir_pair
):
    stored_count = hist_err.shape[0]
    flat_stored = hist_err.astype(jnp.float32).reshape(stored_count, -1)
    all_cols = lax.all_gather(lambda2, "col", axis=0, tiled=True)
    ladder = lax.psum_scatter(
        jnp.dot(all_cols, integrals, preferred_element_type=jnp.float32),
        "row",
        scatter_dimension=0,
        tiled=True,
    )
    denominator = pair_energy(occ_pair, eps_occ)[:, None] - pair_energy(vir_pair, eps_vir)[None, :]
    raw_update = (source_terms + ladder) / denominator
    err_new = raw_update - hist_amp[0].astype(jnp.float32)
    flat_new = err_new.reshape(1, -1)
    stacked = jnp.concatenate([flat_stored, flat_new], axis=0)
    correlation = lax.psum(jnp.dot(stacked, stacked.T, precision=precise), ("row", "col"))
    weights = diis_weights(correlation)
    updated = weights[stored_count] * raw_update
    for k in range(stored_count):
        updated = updated + weights[k] * hist_amp[k].astype(jnp.float32)
    return updated


def solution(mesh):
    placed = (
        P("row", "col"),
        P("col", "row"),
        P("row", "col"),
        P(None, "row", "col"),
        P(None, "row", "col"),
        P(),
        P(),
        P(None, "row"),
        P(None, "col"),
    )
    return jax.shard_map(
        on_device, mesh=mesh, in_specs=placed, out_specs=P("row", "col"), check_vma=False
    )
```

profile of v0, /device:TPU:1, one launch (start us, length us, event | category | flops | bytes accessed | tf_op | source)
XLA Modules:
  0.0 320.9 jit_solution(15406420744793112163)
XLA Ops:
  6.5 0.7 all-gather.3.cloned.1.call-update
  7.3 0.8 fusion.14
  8.0 1.5 select_reduce_fusion
  9.6 1.2 convert_bitcast_fusion
  10.8 54.8 %all-gather.3.cloned.1.call-done = bf16[8,252,2048]{2,1,0:T(8,128)(2,1)} async-done(((bf16[1,252,2048]{2,1,0:T(8,128)(2,1)}), bf16[8,252,2048]{2,1,0:T(8,128)(2,1)}) %all-gather.3.cloned.1.call-update) | async-done | bytes 8257552 | tf_op jit(solution)/shard_map/all_gather | solution.py:42
  65.7 7.5 %reshape.68 = bf16[2016,2048]{1,0:T(8,128)(2,1)} reshape(bf16[8,252,2048]{2,1,0:T(8,128)(2,1)} %all-gather.3.cloned.1.call-done) | data formatting | bytes 16515072
  73.1 14.2 %fusion.18 = f32[2016,1024]{1,0:T(8,128)} fusion(bf16[2016,2048]{1,0:T(8,128)(2,1)} %reshape.68, bf16[2048,1024]{1,0:T(8,128)(2,1)} %param.9), kind=kOutput, calls=%fused_computation.38 | convolution fusion | flops 8455716864 | bytes 20709376 | tf_op jit(solution)/shard_map/dot_general | solution.py:44
  87.4 100.2 %fusion = f32[64,1024]{1,0:T(8,128)S(1)} fusion(f32[2016,1024]{1,0:T(8,128)} %fusion.18), kind=kCustom, calls=%all-reduce-scatter | all-reduce-scatter fusion | flops 2097153 | bytes 8520704
  187.6 0.0 copy-start
  187.6 0.0 copy-start.5
  187.6 0.0 copy-start.4
  187.6 2.3 collective-permute-start
  190.0 0.8 copy.19
  190.8 0.0 copy-start.1
  190.8 0.0 copy-start.2
  190.8 0.6 dynamic-slice.4
  192.0 0.2 select_reduce_fusion.2
  192.2 0.0 collective-permute-done
  192.2 2.0 concatenate.4
  194.2 1.1 fusion.5
  195.3 0.3 copy.20
  195.6 4.5 %fusion.1 = f32[6,6]{0,1:T(8,128)S(1)} fusion(f32[1,64512]{1,0:T(1,128)S(1)} %bitcast.70, f32[5,64512]{1,0:T(8,128)S(1)} %bitcast.68), kind=kOutput, calls=%fused_computation.4 | convolution fusion | flops 28256256 | bytes 1548432 | tf_op jit(solution)/shard_map/dot_general | solution.py:54
  200.1 78.7 %psum.7 = f32[6,6]{0,1:T(8,128)S(1)} all-reduce(f32[6,6]{0,1:T(8,128)S(1)} %fusion.1), channel_id=1, replica_groups=mesh['row'=32,'col'=8] {'row','col'}, use_global_device_ids=true, to_apply=%region_5.6 | all-reduce | flops 36 | bytes 288 | tf_op jit(solution)/shard_map/psum | solution.py:54
  278.8 0.1 copy.17
  278.9 0.5 cholesky.18
  279.4 0.6 compare_reduce_fusion
  280.1 0.6 select_select_fusion
  280.7 0.6 fusion.16
  281.3 0.7 fusion.15
  308.7 0.1 stack.27
  308.7 0.7 fusion.17
  309.4 4.6 %fusion.10 = f32[63,1024]{1,0:T(8,128)} fusion(bf16[5,63,1024]{2,1,0:T(8,128)(2,1)S(1)} %copy-done.2, f32[]{:T(128)} %bitcast.43, f32[]{:T(128)} %bitcast.41, f32[]{:T(128)} %bitcast.39, f32[]{:T(128)} %bitcast.37, f32[]{:T(128)} %bitcast.35, f32[]{:T(128)} %bitcast.34, f32[1024]{0:T(1024)S(1)} %add.47, f32[63]{0:T(128)S(1)} %add.46, ...), kind=kLoop, calls=%fused_computation.16 | loop fusion | flops 1225728 | bytes 1423640 | tf_op jit(solution)/shard_map/add | solution.py:58
  (15 shorter events, 0.1 us)
Async XLA Ops:
  6.5 59.1 %all-gather.3.cloned.1.call-start = ((), (), s32[]{:S(2)}) async-start(), calls=%async_computation | async-start | bytes 9437184 | tf_op jit(solution)/shard_map/all_gather | solution.py:42
  87.4 102.6 %copy-start.3 = (s32[2,63]{1,0:T(2,128)S(1)}, s32[2,63]{1,0:T(2,128)}, u32[]{:S(2)}) copy-start(s32[2,63]{1,0:T(2,128)} %param.16) | copy-start | bytes 1516
  187.6 2.4 copy-start
  187.6 3.2 copy-start.5
  187.6 4.3 %copy-start.4 = (f32[64]{0:T(128)S(1)}, f32[64]{0:T(128)}, u32[]{:S(2)}) copy-start(f32[64]{0:T(128)} %param.14) | copy-start | bytes 772
  187.6 4.5 %collective-permute-start = (f32[31,1024]{1,0:T(8,128)S(1)}, f32[31,1024]{1,0:T(8,128)}, u32[]{:S(2)}, u32[]{:S(2)}) collective-permute-start(f32[31,1024]{1,0:T(8,128)S(1)} %slice.172), channel_id=1, source_target_pairs={{0,8},{8,16},{16,24},{24,32},{32,40},{40,48},{48,56},{56,64},{64,7... | collective-permute-start | bytes 380936
  190.8 118.6 %copy-start.1 = (f32[63,1024]{1,0:T(8,128)S(1)}, f32[63,1024]{1,0:T(8,128)}, u32[]{:S(2)}) copy-start(f32[63,1024]{1,0:T(8,128)} %param.11) | copy-start | bytes 774148
  190.8 118.6 %copy-start.2 = (bf16[5,63,1024]{2,1,0:T(8,128)(2,1)S(1)}, bf16[5,63,1024]{2,1,0:T(8,128)(2,1)}, u32[]{:S(2)}) copy-start(bf16[5,63,1024]{2,1,0:T(8,128)(2,1)} %param.12) | copy-start | bytes 1935364
Sparse Core Ops, SparseCore 0:
  9.2 56.4 all-gather.2
where the time goes:
time: 322 us; the launch traced here: 321 us
  blocking collectives  179 us (56%)
  waiting for transfers between devices  55.6 us (17%)
  between operations  40.7 us (13%)
  matrix products  18.7 us (6%)
  local copies, waits for them, and re-layouts  14.1 us (4%)
  other arithmetic  10.6 us (3%)
    unnamed x1, blocking collectives  100 us
    psum x1, blocking collectives, on_device(): lax.psum(jnp.dot(stacked, stacked.T, precision=precise), ('row', 'col'))  78.7 us
    all_gather x1, waiting for transfers between devices, on_device(): all_cols = lax.all_gather(lambda2, 'col', axis=0, tiled=True)  54.8 us
    dot_general x1, matrix products, on_device(): jnp.dot(all_cols, integrals, preferred_element_type=jnp.float32)  14.2 us
    unnamed x18, local copies, waits for them, and re-layouts  11.2 us
  transfers between devices with their start and end apart: 2, of which 1 were waited for; matrix products, arithmetic and copies ran while one was open for 2% of the time, Pallas kernels for 0%

commit v1 on v0

--- a/solution.py
+++ b/solution.py
@@ -1,9 +1,20 @@
+import functools
 import jax
 import jax.numpy as jnp
 from jax import lax
 from jax.sharding import PartitionSpec as P
 
 precise = lax.Precision.HIGHEST
+
+
+def resolve_the_tables(vals, on_dim):
+    after = jnp.concatenate(
+        jax.lax.all_to_all(jnp.stack([vals] * jax.lax.axis_size("col")), "col", 0, 0), axis=on_dim
+    )
+    return after
+
+
+spread_slices_by_axis = functools.partial(resolve_the_tables, on_dim=0)
 
 
 def pair_energy(pairs, energies):
@@ -39,7 +50,7 @@
 ):
     stored_count = hist_err.shape[0]
     flat_stored = hist_err.astype(jnp.float32).reshape(stored_count, -1)
-    all_cols = lax.all_gather(lambda2, "col", axis=0, tiled=True)
+    all_cols = spread_slices_by_axis(lambda2)
     ladder = lax.psum_scatter(
         jnp.dot(all_cols, integrals, preferred_element_type=jnp.float32),
         "row",

time: 322 us -> 357 us (1.11)
  waiting for transfers between devices: 55.6 us -> 92.8 us
  between operations: 40.7 us -> 27.3 us
  starting transfers between devices: 2.31 us -> 11 us
  local copies, waits for them, and re-layouts: 14.1 us -> 18.9 us
    all_to_all x0 -> x1, waiting for transfers between devices: none -> 92.8 us  [resolve_the_tables(): jax.lax.all_to_all(jnp.stack([vals] * jax.lax.axis_size('col')), 'col', 0...]
    all_gather x1 -> x0, waiting for transfers between devices: 54.8 us -> none  [on_device(): all_cols = lax.all_gather(lambda2, 'col', axis=0, tiled=True)]
    all_to_all x0 -> x1, starting transfers between devices: none -> 8.17 us  [resolve_the_tables(): jax.lax.all_to_all(jnp.stack([vals] * jax.lax.axis_size('col')), 'col', 0...]
    reshape x0 -> x1, local copies, waits for them, and re-layouts: none -> 7.46 us  [resolve_the_tables(): jnp.concatenate(jax.lax.all_to_all(jnp.stack([vals] * jax.lax.axis_size('...]
    unnamed x18 -> x23, local copies, waits for them, and re-layouts: 11.2 us -> 3.7 us
    another operation x0 -> x1, local copies, waits for them, and re-layouts: none -> 5.51 us  [resolve_the_tables(): jnp.stack([vals] * jax.lax.axis_size('col'))]
  transfers between devices with their start and end apart: 2 -> 2, of which waited for: 1 -> 1; matrix products, arithmetic and copies ran while one was open for 2% -> 1% of each run, Pallas kernels for 0% -> 0%
where the time goes in v1:
time: 357 us; the launch traced here: 356 us
  blocking collectives  178 us (50%)
  waiting for transfers between devices  92.8 us (26%)
  between operations  27.3 us (8%)
  local copies, waits for them, and re-layouts  18.9 us (5%)
  matrix products  18.7 us (5%)
  starting transfers between devices  11 us (3%)
  other arithmetic  8.77 us (2%)
    unnamed x1, blocking collectives  99.2 us
    all_to_all x1, waiting for transfers between devices, resolve_the_tables(): jax.lax.all_to_all(jnp.stack([vals] * jax.lax.axis_size('col')), 'col', 0...  92.8 us
    psum x1, blocking collectives, on_device(): lax.psum(jnp.dot(stacked, stacked.T, precision=precise), ('row', 'col'))  79.2 us
    dot_general x1, matrix products, on_device(): jnp.dot(all_cols, integrals, preferred_element_type=jnp.float32)  14.2 us
    all_to_all x1, starting transfers between devices, resolve_the_tables(): jax.lax.all_to_all(jnp.stack([vals] * jax.lax.axis_size('col')), 'col', 0...  8.17 us
    reshape x1, local copies, waits for them, and re-layouts, resolve_the_tables(): jnp.concatenate(jax.lax.all_to_all(jnp.stack([vals] * jax.lax.axis_size('...  7.46 us
  transfers between devices with their start and end apart: 2, of which 1 were waited for; matrix products, arithmetic and copies ran while one was open for 1% of the time, Pallas kernels for 0%

profile of v1, /device:TPU:1, one launch (start us, length us, event | category | flops | bytes accessed | tf_op | source)
XLA Modules:
  0.0 355.9 jit_solution(6870656481076839429)
XLA Ops:
  0.0 5.5 %stack.32 = bf16[8,252,2048]{2,1,0:T(8,128)(2,1)} broadcast(bf16[252,2048]{1,0:T(8,128)(2,1)} %param.10), dimensions={1,2} | broadcast | bytes 9289728 | tf_op jit(solution)/shard_map/stack | solution.py:12
  5.5 8.2 %all-to-all-start = ((bf16[8,252,2048]{2,1,0:T(8,128)(2,1)}), bf16[8,252,2048]{2,1,0:T(8,128)(2,1)}, u32[]{:S(2)}, u32[]{:S(2)}) async-start(bf16[8,252,2048]{2,1,0:T(8,128)(2,1)} %stack.32), calls=%async_computation | async-start | bytes 16777216 | tf_op jit(solution)/shard_map/all_to_all | solution.py:12
  13.7 0.8 select_reduce_fusion
  14.5 0.1 convert_bitcast_fusion
  14.6 92.8 %all-to-all-done = bf16[8,252,2048]{2,1,0:T(8,128)(2,1)} async-done(((bf16[8,252,2048]{2,1,0:T(8,128)(2,1)}), bf16[8,252,2048]{2,1,0:T(8,128)(2,1)}, u32[]{:S(2)}, u32[]{:S(2)}) %all-to-all-start) | async-done | bytes 8257568 | tf_op jit(solution)/shard_map/all_to_all | solution.py:12
  107.4 7.5 %reshape.67 = bf16[2016,2048]{1,0:T(8,128)(2,1)} reshape(bf16[8,252,2048]{2,1,0:T(8,128)(2,1)} %all-to-all-done) | data formatting | bytes 16515072 | tf_op jit(solution)/shard_map/reshape | solution.py:11
  114.9 14.2 %fusion.18 = f32[2016,1024]{1,0:T(8,128)} fusion(bf16[2016,2048]{1,0:T(8,128)(2,1)} %reshape.67, bf16[2048,1024]{1,0:T(8,128)(2,1)} %param.9), kind=kOutput, calls=%fused_computation.38 | convolution fusion | flops 8455716864 | bytes 20709376 | tf_op jit(solution)/shard_map/dot_general | solution.py:55
  129.1 99.2 %fusion = f32[64,1024]{1,0:T(8,128)S(1)} fusion(f32[2016,1024]{1,0:T(8,128)} %fusion.18), kind=kCustom, calls=%all-reduce-scatter | all-reduce-scatter fusion | flops 2097153 | bytes 8520704
  228.3 0.0 copy-start
  228.3 0.0 copy-start.7
  228.3 0.0 copy-start.8
  228.4 2.8 collective-permute-start
  231.2 0.8 copy.19
  232.0 0.0 copy-start.1
  232.0 0.0 copy-start.2
  232.0 0.2 select_reduce_fusion.2
  232.3 0.6 dynamic-slice.4
  233.4 0.0 collective-permute-done
  233.4 2.0 concatenate.4
  235.4 1.1 fusion.5
  236.6 0.3 copy.20
  236.8 4.5 %fusion.1 = f32[6,6]{0,1:T(8,128)S(1)} fusion(f32[1,64512]{1,0:T(1,128)S(1)} %bitcast.68, f32[5,64512]{1,0:T(8,128)S(1)} %bitcast.67), kind=kOutput, calls=%fused_computation.4 | convolution fusion | flops 28256256 | bytes 1548432 | tf_op jit(solution)/shard_map/dot_general | solution.py:65
  241.3 79.2 %psum.7 = f32[6,6]{0,1:T(8,128)S(1)} all-reduce(f32[6,6]{0,1:T(8,128)S(1)} %fusion.1), channel_id=1, replica_groups=mesh['row'=32,'col'=8] {'row','col'}, use_global_device_ids=true, to_apply=%region_5.6 | all-reduce | flops 36 | bytes 288 | tf_op jit(solution)/shard_map/psum | solution.py:65
  320.6 0.1 copy.17
  320.7 0.5 cholesky.18
  321.2 0.6 compare_reduce_fusion
  321.9 0.6 select_select_fusion
  322.5 0.6 fusion.16
  323.1 0.7 fusion.15
  350.4 0.1 stack.39
  350.5 0.7 fusion.17
  351.2 4.6 %fusion.10 = f32[63,1024]{1,0:T(8,128)} fusion(bf16[5,63,1024]{2,1,0:T(8,128)(2,1)S(1)} %copy-done.2, f32[]{:T(128)} %bitcast.42, f32[]{:T(128)} %bitcast.40, f32[]{:T(128)} %bitcast.38, f32[]{:T(128)} %bitcast.36, f32[]{:T(128)} %bitcast.34, f32[]{:T(128)} %bitcast.33, f32[1024]{0:T(1024)S(1)} %add.47, f32[63]{0:T(128)S(1)} %add.46, ...), kind=kLoop, calls=%fused_computation.16 | loop fusion | flops 1225728 | bytes 1423640 | tf_op jit(solution)/shard_map/add | solution.py:69
  (21 shorter events, 0.1 us)
Async XLA Ops:
  5.5 8.2 %copy-start.4 = (s32[2,1024]{1,0:T(2,128)S(1)}, s32[2,1024]{1,0:T(2,128)}, u32[]{:S(2)}) copy-start(s32[2,1024]{1,0:T(2,128)} %param.17) | copy-start | bytes 24580
  5.5 8.2 %copy-start.5 = (f32[800]{0:T(1024)S(1)}, f32[800]{0:T(1024)}, u32[]{:S(2)}) copy-start(f32[800]{0:T(1024)} %param.15) | copy-start | bytes 9604
  5.5 9.0 %copy-start.3 = (bf16[5,63,1024]{2,1,0:T(8,128)(2,1)S(1)}, bf16[5,63,1024]{2,1,0:T(8,128)(2,1)}, u32[]{:S(2)}) copy-start(bf16[5,63,1024]{2,1,0:T(8,128)(2,1)} %param.13) | copy-start | bytes 1935364
  5.5 101.9 %all-to-all-start = ((bf16[8,252,2048]{2,1,0:T(8,128)(2,1)}), bf16[8,252,2048]{2,1,0:T(8,128)(2,1)}, u32[]{:S(2)}, u32[]{:S(2)}) async-start(bf16[8,252,2048]{2,1,0:T(8,128)(2,1)} %stack.32), calls=%async_computation | async-start | bytes 16777216 | tf_op jit(solution)/shard_map/all_to_all | solution.py:12
  129.1 102.0 %copy-start.6 = (s32[2,63]{1,0:T(2,128)S(1)}, s32[2,63]{1,0:T(2,128)}, u32[]{:S(2)}) copy-start(s32[2,63]{1,0:T(2,128)} %param.16) | copy-start | bytes 1516
  228.3 2.9 copy-start
  228.3 3.7 %copy-start.7 = (f32[64]{0:T(128)S(1)}, f32[64]{0:T(128)}, u32[]{:S(2)}) copy-start(f32[64]{0:T(128)} %param.14) | copy-start | bytes 772
  228.3 3.9 %copy-start.8 = (u32[256]{0:T(256)S(1)}, u32[256]{0:T(256)}, u32[]{:S(2)}) copy-start(u32[256]{0:T(256)} %constant.47) | copy-start | bytes 3076
  228.4 5.0 %collective-permute-start = (f32[31,1024]{1,0:T(8,128)S(1)}, f32[31,1024]{1,0:T(8,128)}, u32[]{:S(2)}, u32[]{:S(2)}) collective-permute-start(f32[31,1024]{1,0:T(8,128)S(1)} %slice.172), channel_id=1, source_target_pairs={{0,8},{8,16},{16,24},{24,32},{32,40},{40,48},{48,56},{56,64},{64,7... | collective-permute-start | bytes 380936
  232.0 119.2 %copy-start.1 = (f32[63,1024]{1,0:T(8,128)S(1)}, f32[63,1024]{1,0:T(8,128)}, u32[]{:S(2)}) copy-start(f32[63,1024]{1,0:T(8,128)} %param.11) | copy-start | bytes 774148
  232.0 119.2 %copy-start.2 = (bf16[5,63,1024]{2,1,0:T(8,128)(2,1)S(1)}, bf16[5,63,1024]{2,1,0:T(8,128)(2,1)}, u32[]{:S(2)}) copy-start(bf16[5,63,1024]{2,1,0:T(8,128)(2,1)} %param.12) | copy-start | bytes 1935364
